TPU v7x, 32 devices: a whole 2x2x4 slice. The times are simulated.
32 devices in a mesh: grp: 8 (over y, x, core), blk: 4 (over z).
Axes of the slice: x: 2, y: 2, z: 4, core: 2. Of those that a mesh axis runs over, the one named last changes fastest.
Arguments:
- visual: bfloat16 [24576, 3584], P(('grp', 'blk')), may hold values from -6 to 6
- text_queries: float32 [1024, 3584], P(('grp', 'blk')), may hold values from -100 to 100
- kv_weight: bfloat16 [3584, 1024], replicated, may hold values from -0.09375 to 0.09375
- placement: int32 [3072, 1], P(('grp', 'blk')), may hold values from 0 to 31; in each aligned block of 96 rows (0 to 95, 96 to 191, ...) at most 4 rows name the same one
Outputs:
- attended: float32 [1024, 3584], P(('grp', 'blk'))
Inputs may be any that keep to these rules, and one draw needn't show every extreme that they name: `placement`: among the 96 blocks of one frame owner at most 4 name the same attention owner, a bound that some block reaches; every attention owner is named by some block.
All inputs are finite; a program needn't handle non-finite values.
Results may differ from a plain program's by a relative error of at most 0.0003.
Values sent between devices are 32-bit elements; how exact they have to be, the bound alone decides.
A program may use at most 128 MiB of HBM per device.

v0:
```python
import jax
import jax.numpy as jnp
from jax import lax
from jax.sharding import PartitionSpec as P

HEADS = 28
KV_HEADS = 4


def shifted(block, axis, distance):
    devices = range(lax.axis_size(axis))
    route = [((i - distance) % len(devices), i) for i in devices]
    return lax.ppermute(block, axis, route)


def attend(state, keys_all, valid):
    queries, output, peak, total = state
    nkeys = keys_all.shape[0]
    heads_kv = queries.shape[1]
    head_dim = queries.shape[3]
    stride = min(512, nkeys)
    scale = head_dim ** (-0.5)

    def visit(turn, carry):
        output, peak, total = carry
        start = turn * stride
        piece = lax.dynamic_slice_in_dim(keys_all, start, stride, 0)
        marks = lax.dynamic_slice_in_dim(valid, start, stride, 0) > 0.5
        key_heads = piece[:, : heads_kv * head_dim].reshape(stride, heads_kv, head_dim)
        value_heads = piece[:, heads_kv * head_dim :].reshape(stride, heads_kv, head_dim)
        scores = (
            jnp.einsum("rgjd,kgd->rgjk", queries, key_heads, precision=lax.Precision.HIGHEST)
            * scale
        )
        scores = jnp.where(marks[None, None, None, :], scores, -1e30)
        fresh = jnp.maximum(peak, jnp.max(scores, axis=-1))
        weights = jnp.where(marks[None, None, None, :], jnp.exp(scores - fresh[..., None]), 0.0)
        factor = jnp.exp(peak - fresh)
        total = total * factor + jnp.sum(weights, axis=-1)
        output = output * factor[..., None] + jnp.einsum(
            "rgjk,kgd->rgjd", weights, value_heads, precision=lax.Precision.HIGHEST
        )
        return (output, fresh, total)

    output, peak, total = lax.fori_loop(0, nkeys // stride, visit, (output, peak, total))
    return (queries, output, peak, total)


def start_state(queries):
    return (
        queries,
        jnp.zeros_like(queries),
        jnp.full(queries.shape[:3], -1e30, jnp.float32),
        jnp.zeros(queries.shape[:3], jnp.float32),
    )


def on_device(visual, text_queries, kv_weight, placement):
    kv = jnp.dot(visual, kv_weight, preferred_element_type=jnp.float32)
    width = kv.shape[1]
    head_dim = width // (2 * KV_HEADS)
    group = HEADS // KV_HEADS
    blocks = placement.shape[0]
    block_rows = kv.shape[0] // blocks
    groups_count = lax.axis_size("grp")
    cycle_size = lax.axis_size("blk")
    devices = groups_count * cycle_size
    per_pair = max(2, blocks // devices + 1)
    owner = placement[:, 0]
    index = jnp.arange(blocks, dtype=jnp.int32)
    earlier = (owner[:, None] == owner[None, :]) & (index[None, :] < index[:, None])
    rank = jnp.sum(earlier.astype(jnp.int32), axis=1, dtype=jnp.int32)
    slot = owner * per_pair + rank
    outgoing = (
        jnp.zeros((devices * per_pair, block_rows * width), jnp.float32)
        .at[slot]
        .set(kv.reshape(blocks, block_rows * width))
    )
    marks = jnp.zeros((devices * per_pair, block_rows), jnp.float32).at[slot].set(1.0)
    outgoing = outgoing.reshape(devices, per_pair * block_rows, width)
    marks = marks.reshape(devices, per_pair * block_rows)
    arrived, arrived_marks = (
        lax.all_to_all(outgoing, ("grp", "blk"), split_axis=0, concat_axis=0, tiled=True),
        lax.all_to_all(marks, ("grp", "blk"), split_axis=0, concat_axis=0, tiled=True),
    )
    keys_all = arrived.reshape(-1, width)
    valid = arrived_marks.reshape(-1)
    rows = text_queries.shape[0]
    queries = text_queries.reshape(rows, KV_HEADS, group, head_dim)
    state = attend(start_state(queries), keys_all, valid)

    def turn(step, state):
        moved = shifted(state, "blk", 1)
        return attend(moved, keys_all, valid)

    state = lax.fori_loop(1, cycle_size, turn, state)
    output, peak, total = shifted(state[1:], "blk", 1)
    attended = output / total[..., None]
    return attended.reshape(rows, HEADS * head_dim)


def solution(mesh):
    placed = (P(("grp", "blk"), None), P(("grp", "blk"), None), P(), P(("grp", "blk"), None))
    return jax.shard_map(
        on_device, mesh=mesh, in_specs=placed, out_specs=P(("grp", "blk"), None), check_vma=False
    )
```

profile of v0, /device:TPU:2, one launch (start us, length us, event | category | flops | bytes accessed | tf_op | source)
XLA Modules:
  0.0 281.4 jit_solution(658212625728249639)
XLA Ops:
  3.1 6.1 %all-to-all-start = ((f32[32,1,32]{2,1,0:T(1,128)}), f32[32,1,32]{2,1,0:T(1,128)S(1)}, u32[]{:S(2)}, u32[]{:S(2)}) async-start(f32[32,1,32]{2,1,0:T(1,128)} %bitcast.9), calls=%async_computation | async-start | bytes 32768 | tf_op jit(solution)/shard_map/all_to_all | solution.py:84
  9.2 10.9 %fusion.48 = f32[768,1024]{1,0:T(8,128)} fusion(bf16[768,3584]{1,0:T(8,128)(2,1)} %param.10, bf16[3584,1024]{1,0:T(8,128)(2,1)} %param.12), kind=kOutput, calls=%fused_computation.61 | convolution fusion | flops 5637144576 | bytes 15990784 | tf_op jit(solution)/shard_map/dot_general | solution.py:59
  20.1 2.9 %reshape.78 = f32[96,8192]{1,0:T(8,128)S(1)} reshape(f32[768,1024]{1,0:T(8,128)} %fusion.48) | data formatting | bytes 6291456 | tf_op jit(solution)/shard_map/reshape | solution.py:77
  23.0 4.5 %scatter_custom_fusion.1 = f32[128,8192]{1,0:T(8,128)} fusion(s32[96]{0:T(128)S(1)} %fusion.47, f32[96,8192]{1,0:T(8,128)S(1)} %reshape.78, f32[]{:T(128)} %constant.133.clone.1), kind=kCustom, calls=%fused_computation.49 | custom fusion | bytes 4194308 | tf_op jit(solution)/shard_map/scatter | solution.py:77
  27.5 4.9 %reshape.63 = f32[32,32,1024]{2,1,0:T(8,128)} reshape(f32[128,8192]{1,0:T(8,128)} %scatter_custom_fusion.1) | data formatting | bytes 8388608 | tf_op jit(solution)/shard_map/reshape | solution.py:80
  32.4 5.9 %all-to-all-start.1 = ((f32[32,32,1024]{2,1,0:T(8,128)}), f32[32,32,1024]{2,1,0:T(8,128)}, u32[]{:S(2)}, u32[]{:S(2)}) async-start(f32[32,32,1024]{2,1,0:T(8,128)} %reshape.63), calls=%async_computation.1 | async-start | bytes 8388608 | tf_op jit(solution)/shard_map/all_to_all | solution.py:83
  40.1 88.3 %all-to-all-done.1 = f32[32,32,1024]{2,1,0:T(8,128)} async-done(((f32[32,32,1024]{2,1,0:T(8,128)}), f32[32,32,1024]{2,1,0:T(8,128)}, u32[]{:S(2)}, u32[]{:S(2)}) %all-to-all-start.1) | async-done | bytes 4194336 | tf_op jit(solution)/shard_map/all_to_all | solution.py:83
  128.4 5.4 %copy.37 = f32[1024,1024]{0,1:T(8,128)} copy(f32[1024,1024]{1,0:T(8,128)} %bitcast.10) | data formatting | bytes 8388608
  133.8 15.2 %while.53 = (s32[]{:T(128)}, f32[32,4,7,128]{3,0,2,1:T(8,128)}, f32[32,4,7]{0,2,1:T(8,128)S(1)}, f32[32,4,7]{0,2,1:T(8,128)S(1)}, f32[1024]{0:T(1024)S(1)}, /*in...) while((s32[]{:T(128)}, f32[32,4,7,128]{3,0,2,1:T(8,128)}, ...), condition=%wide.region_6.7_spmd.clone, body=%wide.region_3.6_spmd.clone.sunk | while | flops 1415140224 | bytes 16904448 | solution.py:45
  138.4 2.2 fusion.76
  146.0 2.2 fusion.76
  149.0 116.6 %while.52 = (s32[]{:T(128)}, f32[32,4,7,128]{3,0,2,1:T(8,128)S(1)}, f32[32,4,7,128]{3,0,2,1:T(8,128)}, f32[32,4,7]{0,2,1:T(8,128)S(1)}, f32[32,4,7]{0,2,1:T(8,12...) while((s32[]{:T(128)}, f32[32,4,7,128]{3,0,2,1:T(8,128)S(1)}, ...), condition=%wide.region_12.13_spmd, body=%wide.region_7.12_spmd.sunk | while | flops 1415022848 | bytes 18782792 | solution.py:96
  149.0 5.2 %collective-permute-start = (f32[32,4,7,128]{3,0,2,1:T(8,128)S(1)}, f32[32,4,7,128]{3,0,2,1:T(8,128)S(1)}, u32[]{:S(2)}, u32[]{:S(2)}) collective-permute-start(f32[32,4,7,128]{3,0,2,1:T(8,128)S(1)} %get-tuple-element.695), channel_id=1, source_target_pairs={{3,0},{0,1},{1,2},{2,3},{7,4},{4,5},{5,6},{6,7},{11,8},{8,9},{9,10... | collective-permute-start | bytes 1376264 | tf_op jit(solution)/shard_map/while/body/eval_jaxpr/ppermute | solution.py:13
  154.9 18.4 %collective-permute-done.2 = f32[32,4,7]{0,2,1:T(8,128)S(1)} collective-permute-done((f32[32,4,7]{0,2,1:T(8,128)S(1)}, f32[32,4,7]{0,2,1:T(8,128)S(1)}, u32[]{:S(2)}, u32[]{:S(2)}) %collective-permute-start.2) | collective-permute-done | bytes 3616 | tf_op jit(solution)/shard_map/while/body/eval_jaxpr/ppermute | solution.py:13
  173.5 13.0 %while.54 = (s32[]{:T(128)}, f32[32,4,7,128]{3,0,2,1:T(8,128)S(1)}, f32[32,4,7]{0,2,1:T(8,128)S(1)}, f32[32,4,7]{0,2,1:T(8,128)S(1)}, f32[1024]{0:T(1024)S(1)}, ...) while((s32[]{:T(128)}, f32[32,4,7,128]{3,0,2,1:T(8,128)S(1)}, ...), condition=%wide.region_11.11_spmd, body=%wide.region_8.10_spmd.sunk | while | flops 1415022848 | bytes 13234363 | solution.py:45
  177.8 2.3 fusion.82
  181.9 1.8 bitcast_reduce_fusion.5
  184.3 2.3 fusion.82
  187.4 2.5 collective-permute-start
  192.4 19.8 %collective-permute-done.2 = f32[32,4,7]{0,2,1:T(8,128)S(1)} collective-permute-done((f32[32,4,7]{0,2,1:T(8,128)S(1)}, f32[32,4,7]{0,2,1:T(8,128)S(1)}, u32[]{:S(2)}, u32[]{:S(2)}) %collective-permute-start.2) | collective-permute-done | bytes 3616 | tf_op jit(solution)/shard_map/while/body/eval_jaxpr/ppermute | solution.py:13
  212.6 13.1 %while.54 = (s32[]{:T(128)}, f32[32,4,7,128]{3,0,2,1:T(8,128)S(1)}, f32[32,4,7]{0,2,1:T(8,128)S(1)}, f32[32,4,7]{0,2,1:T(8,128)S(1)}, f32[1024]{0:T(1024)S(1)}, ...) while((s32[]{:T(128)}, f32[32,4,7,128]{3,0,2,1:T(8,128)S(1)}, ...), condition=%wide.region_11.11_spmd, body=%wide.region_8.10_spmd.sunk | while | flops 1415022848 | bytes 13234363 | solution.py:45
  214.4 1.8 bitcast_reduce_fusion.5
  216.8 2.3 fusion.82
  220.9 1.8 bitcast_reduce_fusion.5
  223.4 2.3 fusion.82
  227.8 3.7 %collective-permute-start.3 = (f32[32,4,7]{0,2,1:T(8,128)S(1)}, f32[32,4,7]{0,2,1:T(8,128)S(1)}, u32[]{:S(2)}, u32[]{:S(2)}) collective-permute-start(f32[32,4,7]{0,2,1:T(8,128)S(1)} %get-tuple-element.698), channel_id=1, source_target_pairs={{3,0},{0,1},{1,2},{2,3},{7,4},{4,5},{5,6},{6,7},{11,8},{8,9},{9,10... | collective-permute-start | bytes 10760 | tf_op jit(solution)/shard_map/while/body/eval_jaxpr/ppermute | solution.py:13
  231.5 20.0 %collective-permute-done.2 = f32[32,4,7]{0,2,1:T(8,128)S(1)} collective-permute-done((f32[32,4,7]{0,2,1:T(8,128)S(1)}, f32[32,4,7]{0,2,1:T(8,128)S(1)}, u32[]{:S(2)}, u32[]{:S(2)}) %collective-permute-start.2) | collective-permute-done | bytes 3616 | tf_op jit(solution)/shard_map/while/body/eval_jaxpr/ppermute | solution.py:13
  251.7 13.1 %while.54 = (s32[]{:T(128)}, f32[32,4,7,128]{3,0,2,1:T(8,128)S(1)}, f32[32,4,7]{0,2,1:T(8,128)S(1)}, f32[32,4,7]{0,2,1:T(8,128)S(1)}, f32[1024]{0:T(1024)S(1)}, ...) while((s32[]{:T(128)}, f32[32,4,7,128]{3,0,2,1:T(8,128)S(1)}, ...), condition=%wide.region_11.11_spmd, body=%wide.region_8.10_spmd.sunk | while | flops 1415022848 | bytes 13234363 | solution.py:45
  253.5 1.8 bitcast_reduce_fusion.5
  256.0 2.3 fusion.82
  262.5 2.3 fusion.82
  265.7 14.3 %collective-permute-done.5 = f32[32,4,7]{0,2,1:T(8,128)S(1)} collective-permute-done((f32[32,4,7]{0,2,1:T(8,128)S(1)}, f32[32,4,7]{0,2,1:T(8,128)S(1)}, u32[]{:S(2)}, u32[]{:S(2)}) %collective-permute-start.5) | collective-permute-done | bytes 3616 | tf_op jit(solution)/shard_map/ppermute | solution.py:13
  (111 shorter events, 42.5 us)
Async XLA Ops:
  3.1 29.3 %all-to-all-start = ((f32[32,1,32]{2,1,0:T(1,128)}), f32[32,1,32]{2,1,0:T(1,128)S(1)}, u32[]{:S(2)}, u32[]{:S(2)}) async-start(f32[32,1,32]{2,1,0:T(1,128)} %bitcast.9), calls=%async_computation | async-start | bytes 32768 | tf_op jit(solution)/shard_map/all_to_all | solution.py:84
  32.4 5.9 %copy-start = (f32[32,3584]{1,0:T(8,128)S(1)}, f32[32,3584]{1,0:T(8,128)}, u32[]{:S(2)}) copy-start(f32[32,3584]{1,0:T(8,128)} %param.11) | copy-start | bytes 1376260
  32.4 96.0 %all-to-all-start.1 = ((f32[32,32,1024]{2,1,0:T(8,128)}), f32[32,32,1024]{2,1,0:T(8,128)}, u32[]{:S(2)}, u32[]{:S(2)}) async-start(f32[32,32,1024]{2,1,0:T(8,128)} %reshape.63), calls=%async_computation.1 | async-start | bytes 8388608 | tf_op jit(solution)/shard_map/all_to_all | solution.py:83
  137.3 1.0 copy-start.1
  140.6 0.8 copy-start.2
  145.0 1.0 copy-start.1
  148.2 0.8 copy-start.2
  149.0 24.5 %collective-permute-start = (f32[32,4,7,128]{3,0,2,1:T(8,128)S(1)}, f32[32,4,7,128]{3,0,2,1:T(8,128)S(1)}, u32[]{:S(2)}, u32[]{:S(2)}) collective-permute-start(f32[32,4,7,128]{3,0,2,1:T(8,128)S(1)} %get-tuple-element.695), channel_id=1, source_target_pairs={{3,0},{0,1},{1,2},{2,3},{7,4},{4,5},{5,6},{6,7},{11,8},{8,9},{9,10... | collective-permute-start | bytes 1376264 | tf_op jit(solution)/shard_map/while/body/eval_jaxpr/ppermute | solution.py:13
  154.2 19.3 %collective-permute-start.1 = (f32[32,4,7,128]{3,0,2,1:T(8,128)}, f32[32,4,7,128]{3,0,2,1:T(8,128)S(1)}, u32[]{:S(2)}, u32[]{:S(2)}) collective-permute-start(f32[32,4,7,128]{3,0,2,1:T(8,128)} %get-tuple-element.696), channel_id=1, source_target_pairs={{3,0},{0,1},{1,2},{2,3},{7,4},{4,5},{5,6},{6,7},{11,8},{8,9},{9,10... | collective-permute-start | bytes 1376264 | tf_op jit(solution)/shard_map/while/body/eval_jaxpr/ppermute | solution.py:13
  154.9 18.5 %collective-permute-start.2 = (f32[32,4,7]{0,2,1:T(8,128)S(1)}, f32[32,4,7]{0,2,1:T(8,128)S(1)}, u32[]{:S(2)}, u32[]{:S(2)}) collective-permute-start(f32[32,4,7]{0,2,1:T(8,128)S(1)} %get-tuple-element.697), channel_id=1, source_target_pairs={{3,0},{0,1},{1,2},{2,3},{7,4},{4,5},{5,6},{6,7},{11,8},{8,9},{9,10... | collective-permute-start | bytes 10760 | tf_op jit(solution)/shard_map/while/body/eval_jaxpr/ppermute | solution.py:13
  154.9 18.6 %collective-permute-start.3 = (f32[32,4,7]{0,2,1:T(8,128)S(1)}, f32[32,4,7]{0,2,1:T(8,128)S(1)}, u32[]{:S(2)}, u32[]{:S(2)}) collective-permute-start(f32[32,4,7]{0,2,1:T(8,128)S(1)} %get-tuple-element.698), channel_id=1, source_target_pairs={{3,0},{0,1},{1,2},{2,3},{7,4},{4,5},{5,6},{6,7},{11,8},{8,9},{9,10... | collective-permute-start | bytes 10760 | tf_op jit(solution)/shard_map/while/body/eval_jaxpr/ppermute | solution.py:13
  187.4 25.2 %collective-permute-start = (f32[32,4,7,128]{3,0,2,1:T(8,128)S(1)}, f32[32,4,7,128]{3,0,2,1:T(8,128)S(1)}, u32[]{:S(2)}, u32[]{:S(2)}) collective-permute-start(f32[32,4,7,128]{3,0,2,1:T(8,128)S(1)} %get-tuple-element.695), channel_id=1, source_target_pairs={{3,0},{0,1},{1,2},{2,3},{7,4},{4,5},{5,6},{6,7},{11,8},{8,9},{9,10... | collective-permute-start | bytes 1376264 | tf_op jit(solution)/shard_map/while/body/eval_jaxpr/ppermute | solution.py:13
  190.0 22.6 %collective-permute-start.1 = (f32[32,4,7,128]{3,0,2,1:T(8,128)}, f32[32,4,7,128]{3,0,2,1:T(8,128)S(1)}, u32[]{:S(2)}, u32[]{:S(2)}) collective-permute-start(f32[32,4,7,128]{3,0,2,1:T(8,128)} %get-tuple-element.696), channel_id=1, source_target_pairs={{3,0},{0,1},{1,2},{2,3},{7,4},{4,5},{5,6},{6,7},{11,8},{8,9},{9,10... | collective-permute-start | bytes 1376264 | tf_op jit(solution)/shard_map/while/body/eval_jaxpr/ppermute | solution.py:13
  191.5 20.8 %collective-permute-start.2 = (f32[32,4,7]{0,2,1:T(8,128)S(1)}, f32[32,4,7]{0,2,1:T(8,128)S(1)}, u32[]{:S(2)}, u32[]{:S(2)}) collective-permute-start(f32[32,4,7]{0,2,1:T(8,128)S(1)} %get-tuple-element.697), channel_id=1, source_target_pairs={{3,0},{0,1},{1,2},{2,3},{7,4},{4,5},{5,6},{6,7},{11,8},{8,9},{9,10... | collective-permute-start | bytes 10760 | tf_op jit(solution)/shard_map/while/body/eval_jaxpr/ppermute | solution.py:13
  191.7 20.9 %collective-permute-start.3 = (f32[32,4,7]{0,2,1:T(8,128)S(1)}, f32[32,4,7]{0,2,1:T(8,128)S(1)}, u32[]{:S(2)}, u32[]{:S(2)}) collective-permute-start(f32[32,4,7]{0,2,1:T(8,128)S(1)} %get-tuple-element.698), channel_id=1, source_target_pairs={{3,0},{0,1},{1,2},{2,3},{7,4},{4,5},{5,6},{6,7},{11,8},{8,9},{9,10... | collective-permute-start | bytes 10760 | tf_op jit(solution)/shard_map/while/body/eval_jaxpr/ppermute | solution.py:13
  226.5 25.2 %collective-permute-start = (f32[32,4,7,128]{3,0,2,1:T(8,128)S(1)}, f32[32,4,7,128]{3,0,2,1:T(8,128)S(1)}, u32[]{:S(2)}, u32[]{:S(2)}) collective-permute-start(f32[32,4,7,128]{3,0,2,1:T(8,128)S(1)} %get-tuple-element.695), channel_id=1, source_target_pairs={{3,0},{0,1},{1,2},{2,3},{7,4},{4,5},{5,6},{6,7},{11,8},{8,9},{9,10... | collective-permute-start | bytes 1376264 | tf_op jit(solution)/shard_map/while/body/eval_jaxpr/ppermute | solution.py:13
  226.6 25.2 %collective-permute-start.1 = (f32[32,4,7,128]{3,0,2,1:T(8,128)}, f32[32,4,7,128]{3,0,2,1:T(8,128)S(1)}, u32[]{:S(2)}, u32[]{:S(2)}) collective-permute-start(f32[32,4,7,128]{3,0,2,1:T(8,128)} %get-tuple-element.696), channel_id=1, source_target_pairs={{3,0},{0,1},{1,2},{2,3},{7,4},{4,5},{5,6},{6,7},{11,8},{8,9},{9,10... | collective-permute-start | bytes 1376264 | tf_op jit(solution)/shard_map/while/body/eval_jaxpr/ppermute | solution.py:13
  227.2 24.3 %collective-permute-start.2 = (f32[32,4,7]{0,2,1:T(8,128)S(1)}, f32[32,4,7]{0,2,1:T(8,128)S(1)}, u32[]{:S(2)}, u32[]{:S(2)}) collective-permute-start(f32[32,4,7]{0,2,1:T(8,128)S(1)} %get-tuple-element.697), channel_id=1, source_target_pairs={{3,0},{0,1},{1,2},{2,3},{7,4},{4,5},{5,6},{6,7},{11,8},{8,9},{9,10... | collective-permute-start | bytes 10760 | tf_op jit(solution)/shard_map/while/body/eval_jaxpr/ppermute | solution.py:13
  227.8 24.0 %collective-permute-start.3 = (f32[32,4,7]{0,2,1:T(8,128)S(1)}, f32[32,4,7]{0,2,1:T(8,128)S(1)}, u32[]{:S(2)}, u32[]{:S(2)}) collective-permute-start(f32[32,4,7]{0,2,1:T(8,128)S(1)} %get-tuple-element.698), channel_id=1, source_target_pairs={{3,0},{0,1},{1,2},{2,3},{7,4},{4,5},{5,6},{6,7},{11,8},{8,9},{9,10... | collective-permute-start | bytes 10760 | tf_op jit(solution)/shard_map/while/body/eval_jaxpr/ppermute | solution.py:13
  265.6 14.4 %collective-permute-start.4 = (f32[32,4,7,128]{3,0,2,1:T(8,128)}, f32[32,4,7,128]{3,0,2,1:T(8,128)S(1)}, u32[]{:S(2)}, u32[]{:S(2)}) collective-permute-start(f32[32,4,7,128]{3,0,2,1:T(8,128)} %get-tuple-element.298), channel_id=1, source_target_pairs={{3,0},{0,1},{1,2},{2,3},{7,4},{4,5},{5,6},{6,7},{11,8},{8,9},{9,10... | collective-permute-start | bytes 1376264 | tf_op jit(solution)/shard_map/ppermute | solution.py:13
  265.7 14.3 %collective-permute-start.5 = (f32[32,4,7]{0,2,1:T(8,128)S(1)}, f32[32,4,7]{0,2,1:T(8,128)S(1)}, u32[]{:S(2)}, u32[]{:S(2)}) collective-permute-start(f32[32,4,7]{0,2,1:T(8,128)S(1)} %get-tuple-element.299), channel_id=1, source_target_pairs={{3,0},{0,1},{1,2},{2,3},{7,4},{4,5},{5,6},{6,7},{11,8},{8,9},{9,10... | collective-permute-start | bytes 10760 | tf_op jit(solution)/shard_map/ppermute | solution.py:13
where the time goes:
time: 282 us; the launch traced here: 281 us
  waiting for transfers between devices  162 us (57%)
  matrix products  43.4 us (15%)
  local copies, waits for them, and re-layouts  39.8 us (14%)
  starting transfers between devices  28.1 us (10%)
  other arithmetic  7.88 us (3%)
    all_to_all x1, waiting for transfers between devices, on_device(): lax.all_to_all(outgoing, ('grp', 'blk'), split_axis=0, concat_axis=0, til...  88.3 us
    ppermute x14, waiting for transfers between devices, shifted(): return lax.ppermute(block, axis, route)  73.3 us
    dot_general x8, matrix products, visit(): jnp.einsum('rgjk,kgd->rgjd', weights, value_heads, precision=lax.Precisio...  18.1 us
    ppermute x14, starting transfers between devices, shifted(): return lax.ppermute(block, axis, route)  16 us
    dot_general x8, matrix products, visit(): jnp.einsum('rgjd,kgd->rgjk', queries, key_heads, precision=lax.Precision....  14.4 us
    slice x8, local copies, waits for them, and re-layouts, visit(): piece[:, :heads_kv * head_dim].reshape(stride, heads_kv, head_dim)  13.7 us
    dot_general x1, matrix products, on_device(): kv = jnp.dot(visual, kv_weight, preferred_element_type=jnp.float32)  10.9 us
    all_to_all x1, starting transfers between devices, on_device(): lax.all_to_all(marks, ('grp', 'blk'), split_axis=0, concat_axis=0, tiled=...  6.13 us
  transfers between devices with their start and end apart: 16, of which 8 were waited for; matrix products, arithmetic and copies ran while one was open for 9% of the time, Pallas kernels for 0%

commit v1 on v0

v1 whole, which is shorter than its diff:
```python
import functools

import jax
import jax.numpy as jnp
from jax import lax
from jax.experimental import pallas as pl
from jax.experimental.pallas import tpu as pltpu
from jax.sharding import PartitionSpec as P

HEADS = 28
KV_HEADS = 4
MESH = pl.DeviceIdType.MESH
F32 = jnp.float32
BF16 = jnp.bfloat16
NT = (((1,), (1,)), ((), ()))


def dot(a, b):
    return jnp.dot(a, b, preferred_element_type=F32)


def split3(x):
    hi = x.astype(BF16)
    rest = x - hi.astype(F32)
    mid = rest.astype(BF16)
    low = (rest - mid.astype(F32)).astype(BF16)
    return hi, mid, low


def kernel(
    n_grp, n_blk, per_seg, group, dim,
    visual_hbm, query_hbm, weight_hbm, place_ref,
    out_ref,
    visual, weight, pieces, outgoing, arrived, queries,
    counts_out, counts_in, bias, kcat_a, kcat_b, v_t, p_hi, p_lo,
    stats_out, stats_in, partial, partial_in,
    load_sem, weight_sem, query_load_sem,
    query_send, query_recv, count_send, count_recv,
    kv_send, kv_recv, stat_send, stat_recv, part_send, part_recv,
):
    me_g = lax.axis_index("grp")
    me_b = lax.axis_index("blk")
    rows = query_hbm.shape[0]
    n_rows = visual.shape[0]
    blocks = place_ref.shape[0]
    block_rows = n_rows // blocks
    seg_rows = per_seg * block_rows
    lanes = n_blk * rows
    kv_heads = KV_HEADS
    scale = dim ** (-0.5)

    query_load = pltpu.make_async_copy(query_hbm, queries.at[me_b], query_load_sem)
    query_load.start()
    visual_load = pltpu.make_async_copy(visual_hbm, visual, load_sem)
    visual_load.start()

    def weight_loads(h):
        slot = h % 2
        return [
            pltpu.make_async_copy(
                weight_hbm.at[:, pl.ds((half * kv_heads + h) * dim, dim)],
                weight.at[slot, :, pl.ds(half * dim, dim)],
                weight_sem.at[slot, half],
            )
            for half in range(2)
        ]

    for h in range(2):
        for copy in weight_loads(h):
            copy.start()

    barrier = pltpu.get_barrier_semaphore()
    for d in range(1, n_grp):
        pl.semaphore_signal(
            barrier, inc=1, device_id={"grp": lax.rem(me_g + d, n_grp)}, device_id_type=MESH
        )
    for e in range(1, n_blk):
        pl.semaphore_signal(
            barrier, inc=1, device_id={"blk": lax.rem(me_b + e, n_blk)}, device_id_type=MESH
        )
    pl.semaphore_wait(barrier, n_grp + n_blk - 2)

    query_load.wait()
    query_copies = []
    for e in range(1, n_blk):
        copy = pltpu.make_async_remote_copy(
            src_ref=queries.at[me_b],
            dst_ref=queries.at[me_b],
            send_sem=query_send.at[e],
            recv_sem=query_recv.at[e],
            device_id={"blk": lax.rem(me_b + e, n_blk)},
            device_id_type=MESH,
        )
        copy.start()
        query_copies.append(copy)

    owner = place_ref[...]
    seg = jnp.zeros_like(owner)
    for g in range(1, n_grp):
        seg += (owner >= g * n_blk).astype(jnp.int32)
    block_id = lax.broadcasted_iota(jnp.int32, (blocks, n_rows), 0)
    row_id = lax.broadcasted_iota(jnp.int32, (blocks, n_rows), 1)
    first = block_id * block_rows
    within = (row_id >= first) & (row_id < first + block_rows)
    before = row_id >= first + block_rows
    seg_wide = jnp.broadcast_to(seg, (blocks, n_rows))
    row_seg = jnp.sum(jnp.where(within, seg_wide, 0), axis=0, keepdims=True)
    row_in = jnp.sum(jnp.where(within, row_id - first, 0), axis=0, keepdims=True)
    rank = jnp.sum(
        jnp.where(before & (seg_wide == row_seg), 1, 0), axis=0, keepdims=True
    )
    row_slot = row_seg * seg_rows + rank * block_rows + row_in

    for g in range(n_grp):
        count = jnp.sum((seg == g).astype(F32), axis=0, keepdims=True) * block_rows
        counts_out[g] = jnp.broadcast_to(count, counts_out.shape[1:])

    kv_copies = []
    count_copies = []
    visual_load.wait()
    tile = min(256, n_rows)
    for h in range(kv_heads):
        for copy in weight_loads(h):
            copy.wait()

        def project(i, _, slot=h % 2):
            at = pl.ds(pl.multiple_of(i * tile, tile), tile)
            hi, mid, low = split3(dot(visual[at, :], weight[slot]))
            pieces[at, 0 : 2 * dim] = hi
            pieces[at, 2 * dim : 4 * dim] = mid
            pieces[at, 4 * dim : 6 * dim] = low
            return 0

        lax.fori_loop(0, n_rows // tile, project, 0)
        if h + 2 < kv_heads:
            for copy in weight_loads(h + 2):
                copy.start()

        def pack(g, _, h=h):
            slot_id = lax.broadcasted_iota(jnp.int32, (seg_rows, n_rows), 0) + g * seg_rows
            pick = jnp.where(slot_id == row_slot, 1.0, 0.0).astype(BF16)
            both = dot(pick, pieces[...])
            both = both[:, : 2 * dim] + both[:, 2 * dim : 4 * dim] + both[:, 4 * dim :]
            outgoing[2 * h, g] = both[:, :dim]
            outgoing[2 * h + 1, g] = both[:, dim:]
            return 0

        lax.fori_loop(0, n_grp, pack, 0)
        for half in range(2):
            unit = 2 * h + half
            row = []
            for d in range(1, n_grp):
                peer = lax.rem(me_g + d, n_grp)
                copy = pltpu.make_async_remote_copy(
                    src_ref=outgoing.at[unit, peer],
                    dst_ref=arrived.at[unit, d],
                    send_sem=kv_send.at[unit, d],
                    recv_sem=kv_recv.at[unit, d],
                    device_id={"grp": peer},
                    device_id_type=MESH,
                )
                copy.start()
                row.append(copy)
            kv_copies.append(row)
            arrived[unit, 0] = outgoing[unit, me_g]
        if h == 0:
            for d in range(1, n_grp):
                peer = lax.rem(me_g + d, n_grp)
                copy = pltpu.make_async_remote_copy(
                    src_ref=counts_out.at[peer],
                    dst_ref=counts_in.at[d],
                    send_sem=count_send.at[d],
                    recv_sem=count_recv.at[d],
                    device_id={"grp": peer},
                    device_id_type=MESH,
                )
                copy.start()
                count_copies.append(copy)
            counts_in[0] = counts_out[me_g]

    for copy in query_copies:
        copy.wait_recv()
    for copy in count_copies:
        copy.wait_recv()
    key_id = lax.broadcasted_iota(jnp.int32, (seg_rows, 128), 0).astype(F32)
    for d in range(n_grp):
        bias[d * seg_rows : (d + 1) * seg_rows, :] = jnp.where(
            key_id < counts_in[d][0:1, :], 0.0, -1e30
        )

    keys = n_grp * seg_rows
    stat_copies = []
    part_copies = []
    for h in range(kv_heads):
        for copy in kv_copies[2 * h]:
            copy.wait_recv()
        hi, mid, low = split3(arrived[2 * h].reshape(keys, dim))
        kcat_a[:, :dim] = hi
        kcat_a[:, dim:] = mid
        kcat_b[:, :dim] = hi
        kcat_b[:, dim:] = low

        stats_out[h] = jnp.zeros_like(stats_out[h])

        def score(j, _, h=h):
            at = pl.ds(pl.multiple_of((h * group + j) * dim, dim), dim)
            q = queries[:, :, at].reshape(lanes, dim)
            hi, mid, low = split3(q)
            s = lax.dot_general(
                kcat_a[...], jnp.concatenate([hi, hi], 1), NT, preferred_element_type=F32
            )
            t = lax.dot_general(
                kcat_a[...], jnp.concatenate([mid, mid], 1), NT, preferred_element_type=F32
            )
            u = lax.dot_general(
                kcat_b[...], jnp.concatenate([low, hi], 1), NT, preferred_element_type=F32
            )
            b = bias[...]
            if lanes > 128:
                b = jnp.concatenate([b] * (lanes // 128), 1)
            s = (s + (t + u)) * scale + b
            peak = jnp.max(s, axis=0, keepdims=True)
            p = jnp.exp(s - peak)
            total = jnp.sum(p, axis=0, keepdims=True)
            hi = p.astype(BF16)
            p_hi[j] = hi
            p_lo[j] = (p - hi.astype(F32)).astype(BF16)
            stats_out[h, 0, pl.ds(j, 1), :] = peak
            stats_out[h, 1, pl.ds(j, 1), :] = total
            return 0

        lax.fori_loop(0, group, score, 0)
        row = []
        for e in range(1, n_blk):
            copy = pltpu.make_async_remote_copy(
                src_ref=stats_out.at[h],
                dst_ref=stats_in.at[h, e],
                send_sem=stat_send.at[h, e],
                recv_sem=stat_recv.at[h, e],
                device_id={"blk": lax.rem(me_b + e, n_blk)},
                device_id_type=MESH,
            )
            copy.start()
            row.append(copy)
        stat_copies.append(row)

        for copy in kv_copies[2 * h + 1]:
            copy.wait_recv()
        v = arrived[2 * h + 1].reshape(keys, dim).T
        hi = v.astype(BF16)
        v_t[:dim, :] = hi
        v_t[dim:, :] = (v - hi.astype(F32)).astype(BF16)
        for copy in row:
            copy.wait_recv()
        mine = stats_out[h, 0]
        top = mine
        for e in range(1, n_blk):
            top = jnp.maximum(top, stats_in[h, e, 0])
        factor = jnp.exp(mine - top)
        whole = stats_out[h, 1] * factor
        for e in range(1, n_blk):
            whole += stats_in[h, e, 1] * jnp.exp(stats_in[h, e, 0] - top)
        stats_in[h, 0, 0] = factor / whole

        def mix(j, _, h=h):
            o = dot(v_t[...], p_hi[j])
            o = o[:dim] + o[dim:] + dot(v_t[:dim, :], p_lo[j])
            o = (o * stats_in[h, 0, 0, pl.ds(j, 1), :]).T
            at = pl.ds(pl.multiple_of(j * dim, dim), dim)
            partial[h, :, :, at] = o.reshape(n_blk, rows, dim)
            return 0

        lax.fori_loop(0, group, mix, 0)
        row = []
        for e in range(1, n_blk):
            peer = lax.rem(me_b + e, n_blk)
            copy = pltpu.make_async_remote_copy(
                src_ref=partial.at[h, peer],
                dst_ref=partial_in.at[h, e - 1],
                send_sem=part_send.at[h, e],
                recv_sem=part_recv.at[h, e],
                device_id={"blk": peer},
                device_id_type=MESH,
            )
            copy.start()
            row.append(copy)
        part_copies.append(row)

    for h in range(kv_heads):
        for copy in part_copies[h]:
            copy.wait_recv()
        total = partial[h, me_b]
        for e in range(1, n_blk):
            total += partial_in[h, e - 1]
        out_ref[:, h * group * dim : (h + 1) * group * dim] = total

    for row in [query_copies, count_copies] + kv_copies + stat_copies + part_copies:
        for copy in row:
            copy.wait_send()


def on_device(n_grp, n_blk, visual, text_queries, kv_weight, placement):
    n_rows, model = visual.shape
    rows, wide = text_queries.shape
    dim = kv_weight.shape[1] // (2 * KV_HEADS)
    group = wide // dim // KV_HEADS
    blocks = placement.shape[0]
    block_rows = n_rows // blocks
    per_pair = max(2, blocks // (n_grp * n_blk) + 1)
    per_seg = n_blk * per_pair
    seg_rows = per_seg * block_rows
    keys = n_grp * seg_rows
    lanes = n_blk * rows
    heads = KV_HEADS
    units = 2 * heads
    stat_rows = -(-group // 8) * 8
    any_space = pl.BlockSpec(memory_space=pl.ANY)
    in_vmem = pl.BlockSpec(memory_space=pltpu.VMEM)
    dma = pltpu.SemaphoreType.DMA
    return pl.pallas_call(
        functools.partial(kernel, n_grp, n_blk, per_seg, group, dim),
        name="routed_attention",
        out_shape=jax.ShapeDtypeStruct((rows, wide), F32),
        in_specs=[any_space, any_space, any_space, in_vmem],
        out_specs=in_vmem,
        scratch_shapes=[
            pltpu.VMEM((n_rows, model), BF16),
            pltpu.VMEM((2, model, 2 * dim), BF16),
            pltpu.VMEM((n_rows, 6 * dim), BF16),
            pltpu.VMEM((units, n_grp, seg_rows, dim), F32),
            pltpu.VMEM((units, n_grp, seg_rows, dim), F32),
            pltpu.VMEM((n_blk, rows, wide), F32),
            pltpu.VMEM((n_grp, 8, 128), F32),
            pltpu.VMEM((n_grp, 8, 128), F32),
            pltpu.VMEM((keys, 128), F32),
            pltpu.VMEM((keys, 2 * dim), BF16),
            pltpu.VMEM((keys, 2 * dim), BF16),
            pltpu.VMEM((2 * dim, keys), BF16),
            pltpu.VMEM((group, keys, lanes), BF16),
            pltpu.VMEM((group, keys, lanes), BF16),
            pltpu.VMEM((heads, 2, stat_rows, lanes), F32),
            pltpu.VMEM((heads, n_blk, 2, stat_rows, lanes), F32),
            pltpu.VMEM((heads, n_blk, rows, group * dim), F32),
            pltpu.VMEM((heads, n_blk - 1, rows, group * dim), F32),
            dma,
            dma((2, 2)),
            dma,
            dma((n_blk,)),
            dma((n_blk,)),
            dma((n_grp,)),
            dma((n_grp,)),
            dma((units, n_grp)),
            dma((units, n_grp)),
            dma((heads, n_blk)),
            dma((heads, n_blk)),
            dma((heads, n_blk)),
            dma((heads, n_blk)),
        ],
        compiler_params=pltpu.CompilerParams(
            collective_id=0, has_side_effects=True, vmem_limit_bytes=67043328
        ),
    )(visual, text_queries, kv_weight, placement)


def solution(mesh):
    placed = (P(("grp", "blk"), None), P(("grp", "blk"), None), P(), P(("grp", "blk"), None))
    body = functools.partial(on_device, mesh.shape["grp"], mesh.shape["blk"])
    return jax.shard_map(
        body, mesh=mesh, in_specs=placed, out_specs=P(("grp", "blk"), None), check_vma=False
    )
```

time: 282 us -> 117 us (0.41)
  waiting for transfers between devices: 162 us -> 0 us
  Pallas kernels: 0 us -> 113 us
  matrix products: 43.4 us -> 0 us
  local copies, waits for them, and re-layouts: 39.8 us -> 3.19 us
  starting transfers between devices: 28.1 us -> 0 us
  other arithmetic: 7.88 us -> 0 us
    pallas_call x0 -> x1, Pallas kernels: none -> 113 us  [on_device(): pl.pallas_call(functools.partial(kernel, n_grp, n_blk, per_seg, group, di...]
    all_to_all x2 -> x0, waiting for transfers between devices: 88.3 us -> none  [the longest x1 88.3 us: on_device(): lax.all_to_all(outgoing, ('grp', 'blk'), split_axis=0, concat_axis=0, til...]
    ppermute x14 -> x0, waiting for transfers between devices: 73.3 us -> none  [shifted(): return lax.ppermute(block, axis, route)]
    dot_general x17 -> x0, matrix products: 43.4 us -> none  [the longest x8 18.1 us: visit(): jnp.einsum('rgjk,kgd->rgjd', weights, value_heads, precision=lax.Precisio...]
    ppermute x14 -> x0, starting transfers between devices: 16 us -> none  [shifted(): return lax.ppermute(block, axis, route)]
    slice x8 -> x0, local copies, waits for them, and re-layouts: 13.7 us -> none  [visit(): piece[:, :heads_kv * head_dim].reshape(stride, heads_kv, head_dim)]
    all_to_all x2 -> x0, starting transfers between devices: 12 us -> none  [the longest x1 6.13 us: on_device(): lax.all_to_all(marks, ('grp', 'blk'), split_axis=0, concat_axis=0, tiled=...]
    reshape x5 -> x0, local copies, waits for them, and re-layouts: 8.99 us -> none  [the longest x1 4.94 us: on_device(): outgoing = outgoing.reshape(devices, per_pair * block_rows, width)]
  transfers between devices with their start and end apart: 16 -> 0, of which waited for: 8 -> 0; matrix products, arithmetic and copies ran while one was open for 9% -> 0% of each run, Pallas kernels for 0% -> 0%
where the time goes in v1:
time: 117 us; the launch traced here: 116 us
  Pallas kernels  113 us (97%)
  local copies, waits for them, and re-layouts  3.19 us (3%)
    pallas_call x1, Pallas kernels, on_device(): pl.pallas_call(functools.partial(kernel, n_grp, n_blk, per_seg, group, di...  113 us
    unnamed x2, local copies, waits for them, and re-layouts  3.19 us

profile of v1, /device:TPU:2, one launch (start us, length us, event | category | flops | bytes accessed | tf_op | source)
XLA Modules:
  0.0 115.7 jit_solution(5235197841756488498)
XLA Ops:
  0.0 1.4 %copy.5.place_ref = s32[96,1]{1,0:T(8,128)} copy(s32[96,1]{0,1:T(1,128)} %param.7) | data formatting | bytes 768 | tf_op args[3]
  1.4 112.5 %routed_attention.1 = f32[32,3584]{1,0:T(8,128)} custom-call(bf16[768,3584]{1,0:T(8,128)(2,1)} %visual_hbm.1, f32[32,3584]{1,0:T(8,128)} %query_hbm.1, bf16[3584,1024]{1,0:T(8,128)(2,1)} %weight_hbm.1, s32[96,1]{1,0:T(8,128)} %copy.5.place_ref), custom_call_target="tpu_custom_call" | custom-call | tf_op jit(solution)/shard_map/routed_attention/pallas_call | solution.py:320
  113.9 1.8 %copy.7 = f32[32,3584]{1,0:T(8,128)} copy(f32[32,3584]{1,0:T(8,128)} %routed_attention.1) | data formatting | bytes 917504
